TPU v7x, 256 devices: a whole 4x4x8 slice. The times are simulated.
256 devices in a mesh: tok: 8 (over x, core), col: 32 (over y, z).
Axes of the slice: x: 4, y: 4, z: 8, core: 2. Of those that a mesh axis runs over, the one named last changes fastest.
Arguments:
- hidden_in: bfloat16 [2048, 36864], P('tok', 'col'), may hold values from -6 to 6
- down_weight: bfloat16 [4608, 36864], P('col', 'tok'), may hold values from -0.046875 to 0.046875
- keep_mask: int32 [4608, 36864], P('col', 'tok'), may hold values 0 or 1
Outputs:
- layer_out: bfloat16 [2048, 4608], P(('tok', 'col'))
- hessian: float32 [4608, 4608], P('col', 'tok')
All inputs are finite; a program needn't handle non-finite values. No bound on the sum of `keep_mask` on one device may be relied on, other than what follows from the above.
Results may differ from a plain program's by a relative error of at most 0.012.
Values may be sent and summed in bfloat16 or wider, within the bound.
A program may use at most 128 MiB of HBM per device.

v0:
```python
import jax
import jax.numpy as jnp
from jax import lax
from jax.sharding import PartitionSpec as P


def laid_out(pieces, dim):
    lengths = list(pieces.shape[1:])
    lengths[dim] *= pieces.shape[0]
    return jnp.moveaxis(pieces, 0, dim).reshape(lengths)


def from_everyone(x, axis):
    size = lax.axis_size(axis)
    return lax.all_to_all(jnp.broadcast_to(x[None], (size, *x.shape)), axis, 0, 0, tiled=True)


def gathered_copies(x, axis, dim):
    return laid_out(from_everyone(x, axis), dim)


def split_up(x, dim, size):
    before, after = (x.shape[:dim], x.shape[dim + 1 :])
    return jnp.moveaxis(x.reshape(*before, size, -1, *after), dim, 0)


def sent_and_summed(x, axis, dim):
    pieces = split_up(x, dim, lax.axis_size(axis))
    arrived = lax.all_to_all(pieces, axis, split_axis=0, concat_axis=0, tiled=True)
    return arrived.astype(jnp.float32).sum(axis=0)


def contract_rows(left, right):
    return lax.dot_general(
        left, right, (((0,), (0,)), ((), ())), preferred_element_type=jnp.float32
    )


def contract_last(left, right):
    return lax.dot_general(
        left, right, (((1,), (1,)), ((), ())), preferred_element_type=jnp.float32
    )


def body(hidden_in, down_weight, keep_mask):
    pruned = down_weight * keep_mask.astype(down_weight.dtype)
    all_features = lax.all_gather(hidden_in, "col", axis=1, tiled=True)
    summed = contract_last(all_features, lax.all_gather(pruned, "tok", axis=1, tiled=True))
    layer_cols = summed.astype(jnp.bfloat16)
    scaling = 2.0 / (layer_cols.shape[0] * lax.axis_size("tok"))
    whole = gathered_copies(layer_cols, "col", 1)
    share_rows = whole.shape[0] // lax.axis_size("col")
    layer_out = lax.dynamic_slice_in_dim(whole, lax.axis_index("col") * share_rows, share_rows, 0)
    hessian_term = contract_rows(layer_cols, whole)
    hessian = sent_and_summed((hessian_term * scaling).astype(jnp.bfloat16), "tok", 1)
    return (layer_out, hessian)


def solution(mesh):
    in_specs = (P("tok", "col"), P("col", "tok"), P("col", "tok"))
    out_specs = (P(("tok", "col"), None), P("col", "tok"))
    return jax.shard_map(body, mesh=mesh, in_specs=in_specs, out_specs=out_specs, check_vma=False)
```

profile of v0, /device:TPU:1, one launch (start us, length us, event | category | flops | bytes accessed | tf_op | source)
XLA Modules:
  0.0 347.3 jit_solution(11855072798509974966)
XLA Ops:
  7.2 0.0 all-gather.3.cloned.1.call-start
  7.2 3.4 convert_multiply_fusion
  10.7 0.0 all-gather.3.cloned.1.call-update
  10.7 0.0 all-gather.5.cloned.1.call-start
  10.7 0.7 all-gather.5.cloned.1.call-update
  11.4 65.1 %all-gather.3.cloned.1.call-done = bf16[144,36864]{1,0:T(8,128)(2,1)} async-done(((bf16[144,4608]{1,0:T(8,128)(2,1)}), bf16[144,36864]{1,0:T(8,128)(2,1)}) %all-gather.3.cloned.1.call-update) | async-done | bytes 10616848 | tf_op jit(solution)/shard_map/all_gather | solution.py:48
  76.6 152.6 %all-gather.5.cloned.1.call-done = bf16[256,36864]{1,0:T(8,128)(2,1)} async-done(((bf16[256,1152]{1,0:T(8,128)(2,1)}), bf16[256,36864]{1,0:T(8,128)(2,1)}) %all-gather.5.cloned.1.call-update) | async-done | bytes 18874384 | tf_op jit(solution)/shard_map/all_gather | solution.py:47
  229.1 12.8 %convolution_convert_fusion = bf16[144,256]{1,0:T(8,128)(2,1)S(1)} fusion(bf16[144,36864]{1,0:T(8,128)(2,1)} %all-gather.3.cloned.1.call-done, bf16[256,36864]{1,0:T(8,128)(2,1)} %all-gather.5.cloned.1.call-done), kind=kOutput, calls=%fused_computation.5 | convolution fusion | flops 2717945856 | bytes 29564928 | tf_op jit(solution)/shard_map/dot_general | solution.py:40
  241.9 0.2 broadcast_in_dim.2
  242.1 58.9 %all_to_all.10 = bf16[32,256,144]{1,2,0:T(8,128)(2,1)S(1)} all-to-all(bf16[32,256,144]{1,2,0:T(8,128)(2,1)S(1)} %broadcast_in_dim.2), channel_id=1, replica_groups=mesh['tok'=8,'col'=32] {'col'}, dimensions={0} | all-to-all | bytes 4718592 | tf_op jit(solution)/shard_map/all_to_all | solution.py:15
  300.9 2.0 fusion
  303.0 3.7 %reshape.12 = bf16[144,8,576]{2,1,0:T(8,128)(2,1)} reshape(bf16[144,4608]{1,0:T(8,128)(2,1)} %fusion) | data formatting | bytes 2654208 | tf_op jit(solution)/shard_map/reshape | solution.py:24
  306.7 2.7 copy.10
  309.4 9.1 %all-to-all-start.1 = ((bf16[8,144,576]{2,1,0:T(8,128)(2,1)}), bf16[8,144,576]{2,1,0:T(8,128)(2,1)}, u32[]{:S(2)}, u32[]{:S(2)}) async-start(bf16[8,144,576]{2,1,0:T(8,128)(2,1)} %bitcast.13), calls=%async_computation.1 | async-start | bytes 2949120 | tf_op jit(solution)/shard_map/all_to_all | solution.py:29
  318.4 0.4 constant_dynamic-slice_fusion
  318.8 1.0 copy.8
  319.8 18.3 %all-to-all-done.1 = bf16[8,144,576]{2,1,0:T(8,128)(2,1)} async-done(((bf16[8,144,576]{2,1,0:T(8,128)(2,1)}), bf16[8,144,576]{2,1,0:T(8,128)(2,1)}, u32[]{:S(2)}, u32[]{:S(2)}) %all-to-all-start.1) | async-done | bytes 1327136 | tf_op jit(solution)/shard_map/all_to_all | solution.py:29
  338.1 2.4 convert_reduce_fusion
Async XLA Ops:
  7.2 69.4 %all-gather.3.cloned.1.call-start = ((), (), s32[]{:S(2)}) async-start(), calls=%async_computation.2 | async-start | bytes 11943936 | tf_op jit(solution)/shard_map/all_gather | solution.py:48
  10.7 218.5 %all-gather.5.cloned.1.call-start = ((), (), s32[]{:S(2)}) async-start(), calls=%async_computation.3 | async-start | bytes 19464192 | tf_op jit(solution)/shard_map/all_gather | solution.py:47
  309.4 28.7 %all-to-all-start.1 = ((bf16[8,144,576]{2,1,0:T(8,128)(2,1)}), bf16[8,144,576]{2,1,0:T(8,128)(2,1)}, u32[]{:S(2)}, u32[]{:S(2)}) async-start(bf16[8,144,576]{2,1,0:T(8,128)(2,1)} %bitcast.13), calls=%async_computation.1 | async-start | bytes 2949120 | tf_op jit(solution)/shard_map/all_to_all | solution.py:29
Sparse Core Ops, SparseCore 0:
  10.8 65.7 all-gather.2
  79.3 149.8 all-gather.4
where the time goes:
time: 348 us; the launch traced here: 347 us
  waiting for transfers between devices  237 us (68%)
  blocking collectives  58.9 us (17%)
  matrix products  14.8 us (4%)
  between operations  14.1 us (4%)
  starting transfers between devices  9.16 us (3%)
  local copies, waits for them, and re-layouts  7.93 us (2%)
  other arithmetic  5.8 us (2%)
    all_gather x1, waiting for transfers between devices, body(): all_features = lax.all_gather(hidden_in, 'col', axis=1, tiled=True)  153 us
    all_gather x1, waiting for transfers between devices, body(): lax.all_gather(pruned, 'tok', axis=1, tiled=True)  65.1 us
    all_to_all x1, blocking collectives, from_everyone(): lax.all_to_all(jnp.broadcast_to(x[None], (size, *x.shape)), axis, 0, 0, t...  58.9 us
    all_to_all x1, waiting for transfers between devices, sent_and_summed(): lax.all_to_all(pieces, axis, split_axis=0, concat_axis=0, tiled=True)  18.3 us
    dot_general x1, matrix products, contract_last(): lax.dot_general(left, right, (((1,), (1,)), ((), ())), preferred_element_...  12.8 us
    all_to_all x1, starting transfers between devices, sent_and_summed(): lax.all_to_all(pieces, axis, split_axis=0, concat_axis=0, tiled=True)  9.08 us
  transfers between devices with their start and end apart: 3, of which 3 were waited for; matrix products, arithmetic and copies ran while one was open for 0% of the time, Pallas kernels for 0%

commit v1 on v0

v1 whole, which is shorter than its diff:
```python
import jax
import jax.numpy as jnp
from jax import lax
from jax.experimental import pallas as pl
from jax.experimental.pallas import tpu as pltpu
from jax.sharding import PartitionSpec as P

MESH = pl.DeviceIdType.MESH
NX, NY, NZ = 4, 4, 8
BF = jnp.bfloat16
F32 = jnp.float32


def dot_nt(left, right):
    return lax.dot_general(
        left, right, (((1,), (1,)), ((), ())), preferred_element_type=F32
    )


def kernel(
    scaling,
    hid, wgt, msk,
    hout, lout,
    wbuf, mbuf, bsend, bfull, abuf, csend, cown, crecv, zsend, zrecv,
    lacc, lt, rows, cols, ls, lz, lrecv, hsend, hrecv,
    in_sem, a1s, a1r, a2s, a2r, bs, br, rel_s, cs, cr, zs, zr,
    ts, tr, rs, rr, ccs, ccr, l1s, l1r, l2s, l2r, hs, hr,
):
    t = lax.axis_index("tok")
    c = lax.axis_index("col")
    x, k = t // 2, lax.rem(t, 2)
    y, z = c // NZ, lax.rem(c, NZ)
    home = z // 4
    ntok = hid.shape[0]
    half = ntok // 2
    kb = hid.shape[1]
    nb = wgt.shape[0]

    def dev(xx, kk, yy, zz):
        return (xx * 2 + kk, yy * NZ + zz)

    def remote(src, dst, ssem, rsem, to):
        return pltpu.make_async_remote_copy(
            src_ref=src, dst_ref=dst, send_sem=ssem, recv_sem=rsem,
            device_id=to, device_id_type=MESH,
        )

    me = dev(x, k, y, z)

    def arrived(dst, rsem):
        remote(dst, dst, rsem, rsem, me).wait_recv()

    def sent(src, ssem):
        remote(src, src, ssem, ssem, me).wait_send()

    aslot = jnp.where(y == x, 4 + x, y)
    for q in range(2):
        pltpu.make_async_copy(
            hid.at[pl.ds(q * half, half)], abuf.at[aslot, pl.ds(q * half, half)], in_sem.at[q]
        ).start()
    for j in range(4):
        pltpu.make_async_copy(wgt.at[:, pl.ds(j * kb, kb)], wbuf.at[j], in_sem.at[2 + j]).start()
        pltpu.make_async_copy(msk.at[:, pl.ds(j * kb, kb)], mbuf.at[j], in_sem.at[6 + j]).start()

    bar = pltpu.get_barrier_semaphore()
    for f in range(1, 8):
        pl.semaphore_signal(bar, inc=1, device_id=(lax.rem(t + f, 8), c), device_id_type=MESH)
    for d in range(1, NY):
        pl.semaphore_signal(bar, inc=1, device_id=dev(x, k, lax.rem(y + d, NY), z), device_id_type=MESH)
    for d in range(1, NZ):
        for kk in range(2):
            pl.semaphore_signal(bar, inc=1, device_id=dev(x, kk, y, lax.rem(z + d, NZ)), device_id_type=MESH)

    @pl.when(x != y)
    def _():
        pl.semaphore_signal(bar, inc=1, device_id=dev(y, k, x, z), device_id_type=MESH)

    pl.semaphore_wait(bar, jnp.where(x == y, 24, 25))

    def a1(q, d):
        return remote(
            abuf.at[aslot, pl.ds(q * half, half)], abuf.at[aslot, pl.ds(q * half, half)],
            a1s.at[q, d], a1r.at[q, y], dev(x, k, lax.rem(y + d, NY), z),
        )

    def a2(q, ys):
        return remote(
            abuf.at[ys, pl.ds(q * half, half)], abuf.at[4 + x, pl.ds(q * half, half)],
            a2s.at[q, ys], a2r.at[q, x], dev(ys, k, y, z),
        )

    for q in range(2):
        pltpu.make_async_copy(
            hid.at[pl.ds(q * half, half)], abuf.at[aslot, pl.ds(q * half, half)], in_sem.at[q]
        ).wait()
        for d in (2, 1, 3):
            a1(q, d).start()

        @pl.when(y != x)
        def _():
            a2(q, y).start()

    for j in range(4):
        pltpu.make_async_copy(wgt.at[:, pl.ds(j * kb, kb)], wbuf.at[j], in_sem.at[2 + j]).wait()
        pltpu.make_async_copy(msk.at[:, pl.ds(j * kb, kb)], mbuf.at[j], in_sem.at[6 + j]).wait()
        zt = 4 * k + j
        val = wbuf[j] * mbuf[j].astype(BF)
        bsend[j] = val

        @pl.when(zt == z)
        def _():
            bfull[z] = bsend[j]

        @pl.when(zt != z)
        def _():
            remote(bsend.at[j], bfull.at[z], bs.at[j], br.at[z], dev(x, k, y, zt)).start()

    for q in range(2):
        for d in (1, 3, 2):
            ys = lax.rem(y + d, NY)
            slot = jnp.where(ys == x, 4 + x, ys)
            arrived(abuf.at[slot, pl.ds(q * half, half)], a1r.at[q, ys])

            @pl.when(ys != x)
            def _():
                a2(q, ys).start()

    def zpart(i):
        return lax.rem(z + jnp.where(lax.rem(i, 2) == 1, (i + 1) // 2, NZ - i // 2), NZ)

    def relay(i, _):
        zq = zpart(i)

        @pl.when(jnp.logical_or(k != home, i > 0))
        def _():
            arrived(bfull.at[zq], br.at[zq])

        @pl.when(k == home)
        def _():
            remote(bfull.at[zq], bfull.at[zq], rel_s.at[zq], br.at[zq], dev(x, 1 - k, y, z)).start()

        return 0

    lax.fori_loop(0, NZ, relay, 0)

    for q in range(2):
        for e in range(1, NX):
            xs = lax.rem(x + e, NX)
            arrived(abuf.at[4 + xs, pl.ds(q * half, half)], a2r.at[q, xs])

    def product(i, _):
        zq = zpart(i)
        for e in (2, 1, 3, 0):
            x2 = lax.rem(x + e, NX)
            part = dot_nt(bfull[zq], abuf[4 + x2])
            if e == 0:
                cown[zq] = part
            else:
                csend[e - 1, zq] = part.astype(BF)
                remote(
                    csend.at[e - 1, zq], crecv.at[x, zq], cs.at[e - 1, zq], cr.at[x, zq],
                    dev(x2, k, y, z),
                ).start()
        return 0

    lax.fori_loop(0, NZ, product, 0)

    def reduce_x(i):
        zq = zpart(i)
        acc = cown[zq]
        for e in range(1, NX):
            xs = lax.rem(x + e, NX)
            arrived(crecv.at[xs, zq], cr.at[xs, zq])
            acc = acc + crecv[xs, zq].astype(F32)
        return zq, acc

    def reduce_send(i, _):
        zq, acc = reduce_x(i)
        zsend[zq] = acc.astype(BF)
        remote(zsend.at[zq], zrecv.at[z], zs.at[zq], zr.at[z], dev(x, k, y, zq)).start()
        return 0

    lax.fori_loop(1, NZ, reduce_send, 0)
    _, acc = reduce_x(0)
    lacc[...] = acc

    def reduce_z(d, _):
        zq = lax.rem(z + d, NZ)
        arrived(zrecv.at[zq], zr.at[zq])
        lacc[...] += zrecv[zq].astype(F32)
        return 0

    lax.fori_loop(1, NZ, reduce_z, 0)
    lt[...] = lacc[...].astype(BF)

    @pl.when(x != y)
    def _():
        remote(lt, rows.at[y, k], ts, tr, dev(y, k, x, z)).start()

    @pl.when(x == y)
    def _():
        rows[x, k] = lt[...]

    ident = (
        lax.broadcasted_iota(jnp.int32, (ntok, ntok), 0)
        == lax.broadcasted_iota(jnp.int32, (ntok, ntok), 1)
    ).astype(F32).astype(BF)
    ls[...] = dot_nt(ident, lt[...]).reshape(NY, NZ, 8, nb).astype(BF)
    for d in range(1, NZ):
        z2 = lax.rem(z + d, NZ)
        remote(ls.at[:, z2], lz.at[:, z], l1s.at[d], l1r.at[z], dev(x, k, y, z2)).start()
    lz[:, z] = ls[:, z]

    @pl.when(x != y)
    def _():
        arrived(rows.at[x, k], tr)

    def tok_send(f):
        t2 = lax.rem(t + f, 8)
        return remote(rows.at[x, k], rows.at[x, k], rs.at[f], rr.at[t], (t2, c))

    zrow = lax.rem(z, 4) * nb

    def col_send(d):
        return remote(
            rows.at[x, k], cols.at[k, pl.ds(zrow, nb)], ccs.at[d], ccr.at[k, lax.rem(z, 4)],
            dev(x, home, y, lax.rem(z + d, NZ)),
        )

    for d in (4, 3, 5, 2, 6, 1, 7):
        col_send(d).start()

    @pl.when(k != home)
    def _():
        col_send(0).start()

    @pl.when(k == home)
    def _():
        cols[k, pl.ds(zrow, nb)] = rows[x, k]

    for f in (4, 5, 2, 3, 6, 7, 1):
        tok_send(f).start()

    for d in range(1, NZ):
        zq = lax.rem(z + d, NZ)
        arrived(lz.at[:, zq], l1r.at[zq])
    for d in range(1, NY):
        y2 = lax.rem(y + d, NY)
        remote(lz.at[y2], lrecv.at[y], l2s.at[d], l2r.at[y], dev(x, k, y2, z)).start()
    lrecv[y] = lz[y]

    for f in range(1, 8):
        t2 = lax.rem(t + f, 8)
        arrived(rows.at[t2 // 2, lax.rem(t2, 2)], rr.at[t2])
    for kk in range(2):
        for j in range(4):
            @pl.when(jnp.logical_or(4 * k + j != z, k != kk))
            def _():
                arrived(cols.at[kk, pl.ds(j * nb, nb)], ccr.at[kk, j])

    for e in (2, 1, 3, 0):
        y2 = lax.rem(y + e, NY)
        part = dot_nt(rows[y2, 0], cols[0]) + dot_nt(rows[y2, 1], cols[1])
        part = part * scaling
        if e:
            hsend[e - 1] = part.astype(BF)
            remote(hsend.at[e - 1], hrecv.at[y], hs.at[e], hr.at[y], dev(x, k, y2, z)).start()
        else:
            hout[...] = part
    for e in (1, 3, 2):
        ys = lax.rem(y + e, NY)
        arrived(hrecv.at[ys], hr.at[ys])
        hout[...] += hrecv[ys].astype(F32)

    for d in range(1, NY):
        ys = lax.rem(y + d, NY)
        arrived(lrecv.at[ys], l2r.at[ys])
    lout[...] = lrecv[...]

    for q in range(2):
        for d in range(1, NY):
            sent(abuf.at[aslot, pl.ds(q * half, half)], a1s.at[q, d])
        for ys in range(NY):

            @pl.when(ys != x)
            def _():
                sent(abuf.at[ys, pl.ds(q * half, half)], a2s.at[q, ys])

    for j in range(4):

        @pl.when(4 * k + j != z)
        def _():
            sent(bsend.at[j], bs.at[j])

    @pl.when(k == home)
    def _():
        for zq in range(NZ):
            sent(bfull.at[zq], rel_s.at[zq])

    def drain(i, _):
        for e in range(1, NX):
            sent(csend.at[e - 1, i], cs.at[e - 1, i])

        @pl.when(i != z)
        def _():
            sent(zsend.at[i], zs.at[i])

        return 0

    lax.fori_loop(0, NZ, drain, 0)

    @pl.when(x != y)
    def _():
        sent(lt, ts)

    for d in range(1, NZ):
        sent(ls.at[:, 0], l1s.at[d])
        sent(rows.at[x, k], ccs.at[d])
        sent(rows.at[x, k], rs.at[d])
    for d in range(1, NY):
        sent(lz.at[0], l2s.at[d])
        sent(hsend.at[d - 1], hs.at[d])

    @pl.when(k != home)
    def _():
        sent(rows.at[x, k], ccs.at[0])


def body(hidden_in, down_weight, keep_mask):
    ntok, kb = hidden_in.shape
    nb = down_weight.shape[0]
    scaling = 2.0 / (ntok * lax.axis_size("tok"))
    dma = pltpu.SemaphoreType.DMA
    hessian, rows = pl.pallas_call(
        lambda *refs: kernel(scaling, *refs),
        out_shape=(
            jax.ShapeDtypeStruct((nb, 4 * nb), F32),
            jax.ShapeDtypeStruct((NY, NZ, 8, nb), BF),
        ),
        in_specs=[pl.BlockSpec(memory_space=pl.ANY)] * 3,
        out_specs=(pl.BlockSpec(memory_space=pltpu.VMEM),) * 2,
        scratch_shapes=[
            pltpu.VMEM((4, nb, kb), BF),
            pltpu.VMEM((4, nb, kb), jnp.int32),
            pltpu.VMEM((4, nb, kb), BF),
            pltpu.VMEM((NZ, nb, kb), BF),
            pltpu.VMEM((8, ntok, kb), BF),
            pltpu.VMEM((3, NZ, nb, ntok), BF),
            pltpu.VMEM((NZ, nb, ntok), F32),
            pltpu.VMEM((NX, NZ, nb, ntok), BF),
            pltpu.VMEM((NZ, nb, ntok), BF),
            pltpu.VMEM((NZ, nb, ntok), BF),
            pltpu.VMEM((nb, ntok), F32),
            pltpu.VMEM((nb, ntok), BF),
            pltpu.VMEM((NX, 2, nb, ntok), BF),
            pltpu.VMEM((2, 4 * nb, ntok), BF),
            pltpu.VMEM((NY, NZ, 8, nb), BF),
            pltpu.VMEM((NY, NZ, 8, nb), BF),
            pltpu.VMEM((NY, NZ, 8, nb), BF),
            pltpu.VMEM((3, nb, 4 * nb), BF),
            pltpu.VMEM((NY, nb, 4 * nb), BF),
            dma((10,)),
            dma((2, 4)), dma((2, 4)), dma((2, 4)), dma((2, 4)),
            dma((4,)), dma((NZ,)), dma((NZ,)),
            dma((3, NZ)), dma((NX, NZ)), dma((NZ,)), dma((NZ,)),
            dma(()), dma(()),
            dma((8,)), dma((8,)), dma((8,)), dma((2, 4)),
            dma((8,)), dma((8,)), dma((4,)), dma((4,)),
            dma((4,)), dma((4,)),
        ],
        compiler_params=pltpu.CompilerParams(
            collective_id=0, has_side_effects=True, vmem_limit_bytes=60 * 2**20
        ),
    )(hidden_in, down_weight, keep_mask)
    layer_out = rows.transpose(2, 0, 1, 3).reshape(8, NY * NZ * nb)
    return layer_out, hessian


def solution(mesh):
    in_specs = (P("tok", "col"), P("col", "tok"), P("col", "tok"))
    out_specs = (P(("tok", "col"), None), P("col", "tok"))
    return jax.shard_map(body, mesh=mesh, in_specs=in_specs, out_specs=out_specs, check_vma=False)
```

time: 348 us -> 122 us (0.35)
  waiting for transfers between devices: 237 us -> 0 us
  Pallas kernels: 0 us -> 118 us
  blocking collectives: 58.9 us -> 0 us
  matrix products: 14.8 us -> 0 us
  between operations: 14.1 us -> 0.64 us
  starting transfers between devices: 9.16 us -> 0 us
  other arithmetic: 5.8 us -> 0 us
  local copies, waits for them, and re-layouts: 7.93 us -> 3.51 us
    all_gather x2 -> x0, waiting for transfers between devices: 218 us -> none  [the longest x1 153 us: body(): all_features = lax.all_gather(hidden_in, 'col', axis=1, tiled=True)]
    pallas_call x0 -> x1, Pallas kernels: none -> 118 us  [body(): pl.pallas_call(lambda *refs: kernel(scaling, *refs), out_shape=(jax.Shape...]
    all_to_all x1 -> x0, blocking collectives: 58.9 us -> none  [from_everyone(): lax.all_to_all(jnp.broadcast_to(x[None], (size, *x.shape)), axis, 0, 0, t...]
    all_to_all x1 -> x0, waiting for transfers between devices: 18.3 us -> none  [sent_and_summed(): lax.all_to_all(pieces, axis, split_axis=0, concat_axis=0, tiled=True)]
    dot_general x2 -> x0, matrix products: 14.8 us -> none  [the longest x1 12.8 us: contract_last(): lax.dot_general(left, right, (((1,), (1,)), ((), ())), preferred_element_...]
    all_to_all x1 -> x0, starting transfers between devices: 9.08 us -> none  [sent_and_summed(): lax.all_to_all(pieces, axis, split_axis=0, concat_axis=0, tiled=True)]
    reshape x2 -> x1, local copies, waits for them, and re-layouts: 6.4 us -> 0.83 us  [body(): layer_out = rows.transpose(2, 0, 1, 3).reshape(8, NY * NZ * nb)]
  transfers between devices with their start and end apart: 3 -> 0, of which waited for: 3 -> 0; matrix products, arithmetic and copies ran while one was open for 0% -> 0% of each run, Pallas kernels for 0% -> 0%
where the time goes in v1:
time: 122 us
  Pallas kernels  118 us (97%)
  local copies, waits for them, and re-layouts  3.51 us (3%)
    pallas_call x1, Pallas kernels, body(): pl.pallas_call(lambda *refs: kernel(scaling, *refs), out_shape=(jax.Shape...  118 us

profile of v1, /device:TPU:1, one launch (start us, length us, event | category | flops | bytes accessed | tf_op | source)
XLA Modules:
  0.0 122.1 jit_solution(12750518769579919533)
XLA Ops:
  0.6 117.9 %shard_map.50 = (f32[144,576]{1,0:T(8,128)}, bf16[4,8,8,144]{3,2,1,0:T(8,128)(2,1)}) custom-call(bf16[256,1152]{1,0:T(8,128)(2,1)} %refs_0_.1, bf16[144,4608]{1,0:T(8,128)(2,1)} %refs_1_.1, s32[144,4608]{1,0:T(8,128)} %refs_2_.1), custom_call_target="tpu_custom_call" | custom-call | tf_op jit(solution)/shard_map/pallas_call | solution.py:334
  118.6 0.9 copy.5
  119.5 0.8 reshape.7
  120.3 1.7 %copy.7 = f32[144,576]{1,0:T(8,128)} copy(f32[144,576]{1,0:T(8,128)} %get-tuple-element.9) | data formatting | bytes 663552

commit v2 on v1

--- a/solution.py
+++ b/solution.py
@@ -21,9 +21,9 @@
     scaling,
     hid, wgt, msk,
     hout, lout,
-    wbuf, mbuf, bsend, bfull, abuf, csend, cown, crecv, zsend, zrecv,
+    hbuf, wbuf, mbuf, bsend, bfull, abuf, csend, crecv, zsend, zrecv,
     lacc, lt, rows, cols, ls, lz, lrecv, hsend, hrecv,
-    in_sem, a1s, a1r, a2s, a2r, bs, br, rel_s, cs, cr, zs, zr,
+    in_sem, y1s, y1r, xs_s, xs_r, y2s, y2r, y3s, bs, br, rel_s, cs, cr, zs, zr,
     ts, tr, rs, rr, ccs, ccr, l1s, l1r, l2s, l2r, hs, hr,
 ):
     t = lax.axis_index("tok")
@@ -54,13 +54,33 @@
         remote(src, src, ssem, ssem, me).wait_send()
 
     aslot = jnp.where(y == x, 4 + x, y)
-    for q in range(2):
-        pltpu.make_async_copy(
-            hid.at[pl.ds(q * half, half)], abuf.at[aslot, pl.ds(q * half, half)], in_sem.at[q]
-        ).start()
+    holder = y // 2 == k
+    hown = jnp.where(holder, y - 2 * k, 0)
+
+    def load_piece(h, own):
+        rows_h = pl.ds(h * half, half)
+        dst = abuf.at[aslot, rows_h] if own else hbuf.at[rows_h]
+        return pltpu.make_async_copy(hid.at[rows_h], dst, in_sem.at[h])
+
+    def load_weight(j):
+        return (
+            pltpu.make_async_copy(wgt.at[:, pl.ds(j * kb, kb)], wbuf.at[j], in_sem.at[2 + j]),
+            pltpu.make_async_copy(msk.at[:, pl.ds(j * kb, kb)], mbuf.at[j], in_sem.at[6 + j]),
+        )
+
+    for h in range(2):
+
+        @pl.when(y == 2 * k + h)
+        def _():
+            load_piece(h, True).start()
+
+        @pl.when(y != 2 * k + h)
+        def _():
+            load_piece(h, False).start()
+
     for j in range(4):
-        pltpu.make_async_copy(wgt.at[:, pl.ds(j * kb, kb)], wbuf.at[j], in_sem.at[2 + j]).start()
-        pltpu.make_async_copy(msk.at[:, pl.ds(j * kb, kb)], mbuf.at[j], in_sem.at[6 + j]).start()
+        for copy in load_weight(j):
+            copy.start()
 
     bar = pltpu.get_barrier_semaphore()
     for f in range(1, 8):
@@ -77,58 +97,116 @@
 
     pl.semaphore_wait(bar, jnp.where(x == y, 24, 25))
 
-    def a1(q, d):
-        return remote(
-            abuf.at[aslot, pl.ds(q * half, half)], abuf.at[aslot, pl.ds(q * half, half)],
-            a1s.at[q, d], a1r.at[q, y], dev(x, k, lax.rem(y + d, NY), z),
-        )
-
-    def a2(q, ys):
-        return remote(
-            abuf.at[ys, pl.ds(q * half, half)], abuf.at[4 + x, pl.ds(q * half, half)],
-            a2s.at[q, ys], a2r.at[q, x], dev(ys, k, y, z),
-        )
-
-    for q in range(2):
-        pltpu.make_async_copy(
-            hid.at[pl.ds(q * half, half)], abuf.at[aslot, pl.ds(q * half, half)], in_sem.at[q]
-        ).wait()
-        for d in (2, 1, 3):
-            a1(q, d).start()
-
-        @pl.when(y != x)
-        def _():
-            a2(q, y).start()
-
-    for j in range(4):
-        pltpu.make_async_copy(wgt.at[:, pl.ds(j * kb, kb)], wbuf.at[j], in_sem.at[2 + j]).wait()
-        pltpu.make_async_copy(msk.at[:, pl.ds(j * kb, kb)], mbuf.at[j], in_sem.at[6 + j]).wait()
-        zt = 4 * k + j
-        val = wbuf[j] * mbuf[j].astype(BF)
-        bsend[j] = val
-
-        @pl.when(zt == z)
-        def _():
-            bfull[z] = bsend[j]
-
-        @pl.when(zt != z)
-        def _():
-            remote(bsend.at[j], bfull.at[z], bs.at[j], br.at[z], dev(x, k, y, zt)).start()
-
-    for q in range(2):
-        for d in (1, 3, 2):
-            ys = lax.rem(y + d, NY)
-            slot = jnp.where(ys == x, 4 + x, ys)
-            arrived(abuf.at[slot, pl.ds(q * half, half)], a1r.at[q, ys])
-
-            @pl.when(ys != x)
-            def _():
-                a2(q, ys).start()
+    for h in range(2):
+
+        @pl.when(y == 2 * k + h)
+        def _():
+            load_piece(h, True).wait()
+
+        @pl.when(y != 2 * k + h)
+        def _():
+            load_piece(h, False).wait()
+            remote(
+                hbuf.at[pl.ds(h * half, half)], abuf.at[aslot, pl.ds(h * half, half)],
+                y1s.at[h], y1r.at[y], dev(x, k, 2 * k + h, z),
+            ).start()
 
     def zpart(i):
         return lax.rem(z + jnp.where(lax.rem(i, 2) == 1, (i + 1) // 2, NZ - i // 2), NZ)
 
-    def relay(i, _):
+    def prune(i, _):
+        zt = zpart(i)
+
+        @pl.when(zt // 4 == k)
+        def _():
+            j = lax.rem(zt, 4)
+            for copy in load_weight_at(j):
+                copy.wait()
+            bsend[j] = wbuf[j] * mbuf[j].astype(BF)
+
+            @pl.when(zt == z)
+            def _():
+                bfull[z] = bsend[j]
+
+            @pl.when(zt != z)
+            def _():
+                remote(bsend.at[j], bfull.at[z], bs.at[j], br.at[z], dev(x, k, y, zt)).start()
+
+        return 0
+
+    def load_weight_at(j):
+        return (
+            pltpu.make_async_copy(wgt.at[:, pl.ds(0, kb)], wbuf.at[j], in_sem.at[2 + j]),
+            pltpu.make_async_copy(msk.at[:, pl.ds(0, kb)], mbuf.at[j], in_sem.at[6 + j]),
+        )
+
+    lax.fori_loop(0, NZ, prune, 0)
+
+    order = (2, 1, 3, 0)
+    quarter = half // 2
+
+    def piece(slot, h, part=None):
+        if part is None:
+            return abuf.at[slot, pl.ds(h * half, half)]
+        return abuf.at[slot, pl.ds(h * half + part * quarter, quarter)]
+
+    def handed(e, h, part, ssem, up):
+        slot = 4 + lax.rem(x + e, NX)
+        return remote(
+            piece(slot, h, part), piece(slot, h, part), ssem, y2r.at[h, e, part],
+            dev(x, k, lax.rem(y + (1 if up else NY - 1), NY), z),
+        )
+
+    @pl.when(holder)
+    def _():
+        for e in (2, 1, 3):
+            ys = lax.rem(x + NX - e, NX)
+
+            @pl.when(ys != y)
+            def _():
+                arrived(piece(ys, hown), y1r.at[ys])
+
+            remote(piece(ys, hown), piece(4 + x, hown), xs_s.at[e], xs_r.at[x], dev(ys, k, y, z)).start()
+        for e in order:
+            xe = lax.rem(x + e, NX)
+            if e:
+                arrived(piece(4 + xe, hown), xs_r.at[xe])
+            else:
+
+                @pl.when(x != y)
+                def _():
+                    arrived(piece(4 + x, hown), y1r.at[x])
+
+            for m, (part, up) in enumerate(((0, True), (1, False), (1, True), (0, False))):
+                handed(e, hown, part, y2s.at[e, m], up).start()
+
+    def relay_tokens(e):
+        for h in range(2):
+            away = lax.rem(y + NY - 2 * k - h + NY, NY)
+
+            @pl.when(away == 1)
+            def _():
+                arrived(piece(4 + lax.rem(x + e, NX), h, 0), y2r.at[h, e, 0])
+                handed(e, h, 0, y3s.at[e, h], True).start()
+
+            @pl.when(away == 3)
+            def _():
+                arrived(piece(4 + lax.rem(x + e, NX), h, 1), y2r.at[h, e, 1])
+                handed(e, h, 1, y3s.at[e, h], False).start()
+
+    def tokens_here(e):
+        for h in range(2):
+            away = lax.rem(y + NY - 2 * k - h + NY, NY)
+
+            @pl.when(away >= 2)
+            def _():
+                arrived(piece(4 + lax.rem(x + e, NX), h, 0), y2r.at[h, e, 0])
+
+            @pl.when(jnp.logical_or(away == 1, away == 2))
+            def _():
+                arrived(piece(4 + lax.rem(x + e, NX), h, 1), y2r.at[h, e, 1])
+
+    def relay_weights(i, _):
         zq = zpart(i)
 
         @pl.when(jnp.logical_or(k != home, i > 0))
@@ -141,33 +219,32 @@
 
         return 0
 
-    lax.fori_loop(0, NZ, relay, 0)
-
-    for q in range(2):
-        for e in range(1, NX):
-            xs = lax.rem(x + e, NX)
-            arrived(abuf.at[4 + xs, pl.ds(q * half, half)], a2r.at[q, xs])
-
-    def product(i, _):
-        zq = zpart(i)
-        for e in (2, 1, 3, 0):
-            x2 = lax.rem(x + e, NX)
-            part = dot_nt(bfull[zq], abuf[4 + x2])
-            if e == 0:
-                cown[zq] = part
-            else:
-                csend[e - 1, zq] = part.astype(BF)
+    def products(es, lo, hi):
+        def step(i, _):
+            zq = zpart(i)
+            for e in es:
+                x2 = lax.rem(x + e, NX)
+                csend[e - 1, zq] = dot_nt(bfull[zq], abuf[4 + x2]).astype(BF)
                 remote(
                     csend.at[e - 1, zq], crecv.at[x, zq], cs.at[e - 1, zq], cr.at[x, zq],
                     dev(x2, k, y, z),
                 ).start()
-        return 0
-
-    lax.fori_loop(0, NZ, product, 0)
+            return 0
+
+        lax.fori_loop(lo, hi, step, 0)
+
+    for n, e in enumerate(order):
+        relay_tokens(e)
+        lax.fori_loop(2 * n, 2 * n + 2, relay_weights, 0)
+        if n:
+            products(order[:n], 2 * n, 2 * n + 2)
+        tokens_here(e)
+        if e:
+            products((e,), 0, 2 * n + 2)
 
     def reduce_x(i):
         zq = zpart(i)
-        acc = cown[zq]
+        acc = dot_nt(bfull[zq], abuf[4 + x])
         for e in range(1, NX):
             xs = lax.rem(x + e, NX)
             arrived(crecv.at[xs, zq], cr.at[xs, zq])
@@ -277,14 +354,27 @@
         arrived(lrecv.at[ys], l2r.at[ys])
     lout[...] = lrecv[...]
 
-    for q in range(2):
-        for d in range(1, NY):
-            sent(abuf.at[aslot, pl.ds(q * half, half)], a1s.at[q, d])
-        for ys in range(NY):
-
-            @pl.when(ys != x)
-            def _():
-                sent(abuf.at[ys, pl.ds(q * half, half)], a2s.at[q, ys])
+    for h in range(2):
+
+        @pl.when(y != 2 * k + h)
+        def _():
+            sent(hbuf.at[pl.ds(h * half, half)], y1s.at[h])
+
+    @pl.when(holder)
+    def _():
+        for e in (1, 2, 3):
+            sent(piece(4 + x, hown), xs_s.at[e])
+        for e in range(4):
+            for m in range(4):
+                sent(piece(4 + x, hown, 0), y2s.at[e, m])
+
+    for h in range(2):
+        away = lax.rem(y + NY - 2 * k - h + NY, NY)
+
+        @pl.when(jnp.logical_or(away == 1, away == 3))
+        def _():
+            for e in range(4):
+                sent(piece(4 + x, h, 0), y3s.at[e, h])
 
     for j in range(4):
 
@@ -340,13 +430,13 @@
         in_specs=[pl.BlockSpec(memory_space=pl.ANY)] * 3,
         out_specs=(pl.BlockSpec(memory_space=pltpu.VMEM),) * 2,
         scratch_shapes=[
+            pltpu.VMEM((ntok, kb), BF),
             pltpu.VMEM((4, nb, kb), BF),
             pltpu.VMEM((4, nb, kb), jnp.int32),
             pltpu.VMEM((4, nb, kb), BF),
             pltpu.VMEM((NZ, nb, kb), BF),
             pltpu.VMEM((8, ntok, kb), BF),
             pltpu.VMEM((3, NZ, nb, ntok), BF),
-            pltpu.VMEM((NZ, nb, ntok), F32),
             pltpu.VMEM((NX, NZ, nb, ntok), BF),
             pltpu.VMEM((NZ, nb, ntok), BF),
             pltpu.VMEM((NZ, nb, ntok), BF),
@@ -360,7 +450,8 @@
             pltpu.VMEM((3, nb, 4 * nb), BF),
             pltpu.VMEM((NY, nb, 4 * nb), BF),
             dma((10,)),
-            dma((2, 4)), dma((2, 4)), dma((2, 4)), dma((2, 4)),
+            dma((2,)), dma((4,)), dma((4,)), dma((4,)),
+            dma((4, 4)), dma((2, 4, 2)), dma((4, 2)),
             dma((4,)), dma((NZ,)), dma((NZ,)),
             dma((3, NZ)), dma((NX, NZ)), dma((NZ,)), dma((NZ,)),
             dma(()), dma(()),

time: 122 us -> 114 us (0.934)
  the two profiles are of different devices: /device:TPU:1 before, /device:TPU:5 now
where the time goes in v2:
time: 114 us
  Pallas kernels  110 us (96%)
  local copies, waits for them, and re-layouts  3.51 us (3%)
    pallas_call x1, Pallas kernels, body(): pl.pallas_call(lambda *refs: kernel(scaling, *refs), out_shape=(jax.Shape...  110 us

profile of v2, /device:TPU:5, one launch (start us, length us, event | category | flops | bytes accessed | tf_op | source)
XLA Modules:
  0.0 114.1 jit_solution(6207232164007772503)
XLA Ops:
  0.6 109.9 %shard_map.50 = (f32[144,576]{1,0:T(8,128)}, bf16[4,8,8,144]{3,2,1,0:T(8,128)(2,1)}) custom-call(bf16[256,1152]{1,0:T(8,128)(2,1)} %refs_0_.1, bf16[144,4608]{1,0:T(8,128)(2,1)} %refs_1_.1, s32[144,4608]{1,0:T(8,128)} %refs_2_.1), custom_call_target="tpu_custom_call" | custom-call | tf_op jit(solution)/shard_map/pallas_call | solution.py:424
  110.5 0.9 copy.5
  111.5 0.8 reshape.7
  112.3 1.7 %copy.7 = f32[144,576]{1,0:T(8,128)} copy(f32[144,576]{1,0:T(8,128)} %get-tuple-element.9) | data formatting | bytes 663552

commit v3 on v2

v3 whole, which is shorter than its diff:
```python
import jax
import jax.numpy as jnp
from jax import lax
from jax.experimental import pallas as pl
from jax.experimental.pallas import tpu as pltpu
from jax.sharding import PartitionSpec as P

MESH = pl.DeviceIdType.MESH
NX, NY, NZ = 4, 4, 8
BF = jnp.bfloat16
F32 = jnp.float32


def dot_nt(left, right):
    return lax.dot_general(
        left, right, (((1,), (1,)), ((), ())), preferred_element_type=F32
    )


def kernel(
    scaling,
    hid, wgt, msk,
    hout, lout,
    hbuf, wbuf, mbuf, bsend, bfull, abuf, csend, crecv, nrecv, pbuf, zsend, zrecv,
    lacc, lt, rows, cols, ls, lz, lrecv, hsend, hrecv, hacc,
    in_sem, y1s, y1r, xs_s, xs_r, y2s, y2r, y3s, bs, br, rel_s, cs, cr, nr, zs, zr,
    ts, tr, rs, rr, ccs, ccr, l1s, l1r, l2s, l2r, hs, hr,
):
    t = lax.axis_index("tok")
    c = lax.axis_index("col")
    x, k = t // 2, lax.rem(t, 2)
    y, z = c // NZ, lax.rem(c, NZ)
    home = z // 4
    ntok = hid.shape[0]
    half = ntok // 2
    kb = hid.shape[1]
    nb = wgt.shape[0]

    def dev(xx, kk, yy, zz):
        return (xx * 2 + kk, yy * NZ + zz)

    def remote(src, dst, ssem, rsem, to):
        return pltpu.make_async_remote_copy(
            src_ref=src, dst_ref=dst, send_sem=ssem, recv_sem=rsem,
            device_id=to, device_id_type=MESH,
        )

    me = dev(x, k, y, z)

    def arrived(dst, rsem):
        remote(dst, dst, rsem, rsem, me).wait_recv()

    def sent(src, ssem):
        remote(src, src, ssem, ssem, me).wait_send()

    bar = pltpu.get_barrier_semaphore()
    for f in range(1, 8):
        pl.semaphore_signal(bar, inc=1, device_id=(lax.rem(t + f, 8), c), device_id_type=MESH)
    for d in range(1, NY):
        pl.semaphore_signal(bar, inc=1, device_id=dev(x, k, lax.rem(y + d, NY), z), device_id_type=MESH)
    for d in range(1, NZ):
        for kk in range(2):
            pl.semaphore_signal(bar, inc=1, device_id=dev(x, kk, y, lax.rem(z + d, NZ)), device_id_type=MESH)

    @pl.when(x != y)
    def _():
        pl.semaphore_signal(bar, inc=1, device_id=dev(y, k, x, z), device_id_type=MESH)

    aslot = jnp.where(y == x, 4 + x, y)
    holder = y // 2 == k
    hown = jnp.where(holder, y - 2 * k, 0)

    def load_piece(h, own):
        rows_h = pl.ds(h * half, half)
        dst = abuf.at[aslot, rows_h] if own else hbuf.at[rows_h]
        return pltpu.make_async_copy(hid.at[rows_h], dst, in_sem.at[h])

    def load_weight(j):
        return (
            pltpu.make_async_copy(wgt.at[:, pl.ds(j * kb, kb)], wbuf.at[j], in_sem.at[2 + j]),
            pltpu.make_async_copy(msk.at[:, pl.ds(j * kb, kb)], mbuf.at[j], in_sem.at[6 + j]),
        )

    for h in range(2):

        @pl.when(y == 2 * k + h)
        def _():
            load_piece(h, True).start()

        @pl.when(y != 2 * k + h)
        def _():
            load_piece(h, False).start()

    for j in range(4):
        for copy in load_weight(j):
            copy.start()

    def prune(j, _):
        for copy in load_weight_at(j):
            copy.wait()
        bsend[j] = wbuf[j] * mbuf[j].astype(BF)
        return 0

    def load_weight_at(j):
        return (
            pltpu.make_async_copy(wgt.at[:, pl.ds(0, kb)], wbuf.at[j], in_sem.at[2 + j]),
            pltpu.make_async_copy(msk.at[:, pl.ds(0, kb)], mbuf.at[j], in_sem.at[6 + j]),
        )

    lax.fori_loop(0, 4, prune, 0)

    pl.semaphore_wait(bar, jnp.where(x == y, 24, 25))

    quarter = half // 2

    for h in range(2):

        @pl.when(y == 2 * k + h)
        def _():
            load_piece(h, True).wait()

        @pl.when(y != 2 * k + h)
        def _():
            load_piece(h, False).wait()
    for part in range(2):
        for h in range(2):

            @pl.when(y != 2 * k + h)
            def _():
                rows_p = pl.ds(h * half + part * quarter, quarter)
                remote(
                    hbuf.at[rows_p], abuf.at[aslot, rows_p],
                    y1s.at[h, part], y1r.at[y, part], dev(x, k, 2 * k + h, z),
                ).start()

    def zpart(i):
        i = jnp.int32(i)
        return lax.rem(z + jnp.where(lax.rem(i, 2) == 1, (i + 1) // 2, NZ - i // 2), NZ)

    def place(d):
        return jnp.where(d == 0, 0, jnp.where(d <= 4, 2 * d - 1, 2 * (NZ - d)))

    def hand_out(i, _):
        zt = zpart(i)

        @pl.when(zt // 4 == k)
        def _():
            j = lax.rem(zt, 4)

            @pl.when(zt == z)
            def _():
                bfull[0] = bsend[j]

            @pl.when(zt != z)
            def _():
                slot = place(lax.rem(z + NZ - zt, NZ))
                remote(bsend.at[j], bfull.at[slot], bs.at[j], br.at[slot], dev(x, k, y, zt)).start()

        return 0

    lax.fori_loop(0, NZ, hand_out, 0)

    order = (2, 1, 3, 0)

    def piece(slot, h, part=None):
        if part is None:
            return abuf.at[slot, pl.ds(h * half, half)]
        return abuf.at[slot, pl.ds(h * half + part * quarter, quarter)]

    def handed(e, h, part, ssem, up):
        slot = 4 + lax.rem(x + e, NX)
        return remote(
            piece(slot, h, part), piece(slot, h, part), ssem, y2r.at[h, e, part],
            dev(x, k, lax.rem(y + (1 if up else NY - 1), NY), z),
        )

    @pl.when(holder)
    def _():
        for part in range(2):
            for e in (2, 1, 3):
                ys = lax.rem(x + NX - e, NX)

                @pl.when(ys != y)
                def _():
                    arrived(piece(ys, hown, part), y1r.at[ys, part])

                remote(
                    piece(ys, hown, part), piece(4 + x, hown, part),
                    xs_s.at[e, part], xs_r.at[x, part], dev(ys, k, y, z),
                ).start()
        for e in order:
            xe = lax.rem(x + e, NX)
            for part in range(2):
                if e:
                    arrived(piece(4 + xe, hown, part), xs_r.at[xe, part])
                else:

                    @pl.when(x != y)
                    def _():
                        arrived(piece(4 + x, hown, part), y1r.at[x, part])

                for up in (part == 0, part == 1):
                    handed(e, hown, part, y2s.at[e, part, int(up)], up).start()

    def relay_tokens(e):
        for h in range(2):
            away = lax.rem(y + NY - 2 * k - h + NY, NY)

            @pl.when(away == 1)
            def _():
                arrived(piece(4 + lax.rem(x + e, NX), h, 0), y2r.at[h, e, 0])
                handed(e, h, 0, y3s.at[e, h], True).start()

            @pl.when(away == 3)
            def _():
                arrived(piece(4 + lax.rem(x + e, NX), h, 1), y2r.at[h, e, 1])
                handed(e, h, 1, y3s.at[e, h], False).start()

    def tokens_here(e):
        for h in range(2):
            away = lax.rem(y + NY - 2 * k - h + NY, NY)

            @pl.when(away >= 2)
            def _():
                arrived(piece(4 + lax.rem(x + e, NX), h, 0), y2r.at[h, e, 0])

            @pl.when(jnp.logical_or(away == 1, away == 2))
            def _():
                arrived(piece(4 + lax.rem(x + e, NX), h, 1), y2r.at[h, e, 1])

    def relay_weights(i, _):
        @pl.when(jnp.logical_or(k != home, i > 0))
        def _():
            arrived(bfull.at[i], br.at[i])

        @pl.when(k == home)
        def _():
            remote(bfull.at[i], bfull.at[i], rel_s.at[i], br.at[i], dev(x, 1 - k, y, z)).start()

        return 0

    def product(e, lo, hi):
        left = bfull[lo:hi].reshape((hi - lo) * nb, kb)
        return dot_nt(left, abuf[4 + lax.rem(x + e, NX)]).reshape(hi - lo, nb, ntok)

    via_up = (0, 2, 4, 6, 7)

    def products(e, lo, hi, order=None):
        pbuf[lo:hi] = product(e, lo, hi)
        for i in order or range(lo, hi):
            src, ssem = csend.at[e - 1, i], cs.at[e - 1, i]
            if e == 2:
                csend[1, i] = pbuf[i].astype(BF)
                to = lax.rem(x + (1 if i in via_up else NX - 1), NX)
                remote(src, nrecv.at[i], ssem, nr.at[i], dev(to, k, y, z)).start()
                continue
            if (i in via_up) == (e == 1):
                arrived(nrecv.at[i], nr.at[i])
                csend[e - 1, i] = (pbuf[i] + nrecv[i].astype(F32)).astype(BF)
            else:
                csend[e - 1, i] = pbuf[i].astype(BF)
            remote(
                src, crecv.at[e // 2, i], ssem, cr.at[e // 2, i], dev(lax.rem(x + e, NX), k, y, z)
            ).start()

    def weights(lo, hi):
        lax.fori_loop(lo, hi, relay_weights, 0)

    relay_tokens(2)
    weights(0, 3)
    relay_tokens(1)
    tokens_here(2)
    products(2, 0, 3)
    weights(3, 5)
    products(2, 3, 5)
    relay_tokens(3)
    weights(5, 7)
    products(2, 5, 7)
    tokens_here(1)
    products(1, 0, 7, order=(1, 2, 3, 4, 5, 6, 0))
    relay_tokens(0)
    tokens_here(3)
    products(3, 0, 7, order=(1, 2, 3, 4, 5, 6, 0))
    tokens_here(0)
    pbuf[0:7] = product(0, 0, 7)

    def reduce_x(i):
        for side in range(2):
            arrived(crecv.at[side, i], cr.at[side, i])
        return pbuf[i] + crecv[0, i].astype(F32) + crecv[1, i].astype(F32)

    def reduce_send(i):
        zq = zpart(i)
        acc = reduce_x(i).astype(BF)
        for h in range(2):
            zsend[h, zq] = acc[:, h * half : (h + 1) * half]
            remote(
                zsend.at[h, zq], zrecv.at[h, z], zs.at[h, zq], zr.at[h, z], dev(x, k, y, zq)
            ).start()

    reduce_send(1)
    weights(7, 8)
    products(2, 7, 8)
    products(3, 7, 8)
    reduce_send(2)
    reduce_send(3)
    reduce_send(4)
    products(1, 7, 8)
    pbuf[7] = product(0, 7, 8)[0]
    reduce_send(5)
    reduce_send(6)
    reduce_send(7)
    acc = reduce_x(0)
    for h in range(2):
        lacc[h] = acc[:, h * half : (h + 1) * half]

    def reduce_z(h):
        lanes = pl.ds(h * half, half)

        def step(d, _):
            zq = lax.rem(z + d, NZ)
            arrived(zrecv.at[h, zq], zr.at[h, zq])
            lacc[h] += zrecv[h, zq].astype(F32)
            return 0

        lax.fori_loop(1, NZ, step, 0)
        lt[:, lanes] = lacc[h].astype(BF)

        @pl.when(x != y)
        def _():
            remote(lt.at[:, lanes], rows.at[y, k, :, lanes], ts.at[h], tr.at[h], dev(y, k, x, z)).start()

        @pl.when(x == y)
        def _():
            rows[x, k, :, lanes] = lt[:, lanes]

    zrow = lax.rem(z, 4) * nb

    def tok_send(f, h):
        t2 = lax.rem(t + f, 8)
        mine = rows.at[x, k, :, pl.ds(h * half, half)]
        return remote(mine, mine, rs.at[h, f], rr.at[h, t], (t2, c))

    def col_send(d, h):
        lanes = pl.ds(h * half, half)
        return remote(
            rows.at[x, k, :, lanes], cols.at[k, pl.ds(zrow, nb), lanes],
            ccs.at[h, d], ccr.at[h, k, lax.rem(z, 4)],
            dev(x, home, y, lax.rem(z + d, NZ)),
        )

    def spread(h):
        lanes = pl.ds(h * half, half)

        @pl.when(x != y)
        def _():
            arrived(rows.at[x, k, :, lanes], tr.at[h])

        for d in (4, 3, 5, 2, 6, 1, 7):
            col_send(d, h).start()

        @pl.when(k != home)
        def _():
            col_send(0, h).start()

        @pl.when(k == home)
        def _():
            cols[k, pl.ds(zrow, nb), lanes] = rows[x, k, :, lanes]

        for f in (4, 5, 2, 3, 6, 7, 1):
            tok_send(f, h).start()

    reduce_z(0)
    reduce_z(1)
    spread(0)

    ident = (
        lax.broadcasted_iota(jnp.int32, (ntok, ntok), 0)
        == lax.broadcasted_iota(jnp.int32, (ntok, ntok), 1)
    ).astype(F32).astype(BF)
    ls[...] = dot_nt(ident, lt[...]).reshape(NY, NZ, 8, nb).astype(BF)
    for d in range(1, NZ):
        z2 = lax.rem(z + d, NZ)
        remote(ls.at[:, z2], lz.at[:, z], l1s.at[d], l1r.at[z], dev(x, k, y, z2)).start()
    lz[:, z] = ls[:, z]

    spread(1)

    for d in range(1, NZ):
        zq = lax.rem(z + d, NZ)
        arrived(lz.at[:, zq], l1r.at[zq])
    for d in range(1, NY):
        y2 = lax.rem(y + d, NY)
        remote(lz.at[y2], lrecv.at[y], l2s.at[d], l2r.at[y], dev(x, k, y2, z)).start()
    lrecv[y] = lz[y]

    for f in range(1, 8):
        t2 = lax.rem(t + f, 8)
        for h in range(2):
            arrived(rows.at[t2 // 2, lax.rem(t2, 2), :, pl.ds(h * half, half)], rr.at[h, t2])
    for kk in range(2):
        for j in range(4):
            @pl.when(jnp.logical_or(4 * k + j != z, k != kk))
            def _():
                for h in range(2):
                    arrived(cols.at[kk, pl.ds(j * nb, nb), pl.ds(h * half, half)], ccr.at[h, kk, j])

    part = sum(dot_nt(rows[:, kk].reshape(NY * nb, ntok), cols[kk]) for kk in range(2))
    hacc[...] = (part * scaling).reshape(NY, nb, NY * nb)
    for e in (2, 1, 3):
        y2 = lax.rem(y + e, NY)
        hsend[e - 1] = hacc[y2].astype(BF)
        remote(hsend.at[e - 1], hrecv.at[y], hs.at[e], hr.at[y], dev(x, k, y2, z)).start()
    hout[...] = hacc[y]
    for e in (1, 3, 2):
        ys = lax.rem(y + e, NY)
        arrived(hrecv.at[ys], hr.at[ys])
        hout[...] += hrecv[ys].astype(F32)

    for d in range(1, NY):
        ys = lax.rem(y + d, NY)
        arrived(lrecv.at[ys], l2r.at[ys])
    lout[...] = lrecv[...]

    for h in range(2):

        @pl.when(y != 2 * k + h)
        def _():
            for part in range(2):
                sent(hbuf.at[pl.ds(0, quarter)], y1s.at[h, part])

    @pl.when(holder)
    def _():
        for e in (1, 2, 3):
            for part in range(2):
                sent(piece(4 + x, hown, 0), xs_s.at[e, part])
        for e in range(4):
            for m in range(4):
                sent(piece(4 + x, hown, 0), y2s.at[e, m // 2, m % 2])

    for h in range(2):
        away = lax.rem(y + NY - 2 * k - h + NY, NY)

        @pl.when(jnp.logical_or(away == 1, away == 3))
        def _():
            for e in range(4):
                sent(piece(4 + x, h, 0), y3s.at[e, h])

    for j in range(4):

        @pl.when(4 * k + j != z)
        def _():
            sent(bsend.at[j], bs.at[j])

    @pl.when(k == home)
    def _():
        for zq in range(NZ):
            sent(bfull.at[zq], rel_s.at[zq])

    def drain(i, _):
        for e in (1, 2, 3):
            sent(csend.at[e - 1, i], cs.at[e - 1, i])
        for h in range(2):
            @pl.when(i != z)
            def _():
                sent(zsend.at[h, i], zs.at[h, i])

        return 0

    lax.fori_loop(0, NZ, drain, 0)

    piece_h = rows.at[x, k, :, pl.ds(0, half)]
    for h in range(2):

        @pl.when(x != y)
        def _():
            sent(piece_h, ts.at[h])

        for d in range(1, NZ):
            sent(piece_h, ccs.at[h, d])
            sent(piece_h, rs.at[h, d])

        @pl.when(k != home)
        def _():
            sent(piece_h, ccs.at[h, 0])

    for d in range(1, NZ):
        sent(ls.at[:, 0], l1s.at[d])
    for d in range(1, NY):
        sent(lz.at[0], l2s.at[d])
        sent(hsend.at[d - 1], hs.at[d])


def body(hidden_in, down_weight, keep_mask):
    ntok, kb = hidden_in.shape
    nb = down_weight.shape[0]
    scaling = 2.0 / (ntok * lax.axis_size("tok"))
    dma = pltpu.SemaphoreType.DMA
    hessian, rows = pl.pallas_call(
        lambda *refs: kernel(scaling, *refs),
        out_shape=(
            jax.ShapeDtypeStruct((nb, 4 * nb), F32),
            jax.ShapeDtypeStruct((NY, NZ, 8, nb), BF),
        ),
        in_specs=[pl.BlockSpec(memory_space=pl.ANY)] * 3,
        out_specs=(pl.BlockSpec(memory_space=pltpu.VMEM),) * 2,
        scratch_shapes=[
            pltpu.VMEM((ntok, kb), BF),
            pltpu.VMEM((4, nb, kb), BF),
            pltpu.VMEM((4, nb, kb), jnp.int32),
            pltpu.VMEM((4, nb, kb), BF),
            pltpu.VMEM((NZ, nb, kb), BF),
            pltpu.VMEM((8, ntok, kb), BF),
            pltpu.VMEM((3, NZ, nb, ntok), BF),
            pltpu.VMEM((2, NZ, nb, ntok), BF),
            pltpu.VMEM((NZ, nb, ntok), BF),
            pltpu.VMEM((NZ, nb, ntok), F32),
            pltpu.VMEM((2, NZ, nb, ntok // 2), BF),
            pltpu.VMEM((2, NZ, nb, ntok // 2), BF),
            pltpu.VMEM((2, nb, ntok // 2), F32),
            pltpu.VMEM((nb, ntok), BF),
            pltpu.VMEM((NX, 2, nb, ntok), BF),
            pltpu.VMEM((2, 4 * nb, ntok), BF),
            pltpu.VMEM((NY, NZ, 8, nb), BF),
            pltpu.VMEM((NY, NZ, 8, nb), BF),
            pltpu.VMEM((NY, NZ, 8, nb), BF),
            pltpu.VMEM((3, nb, 4 * nb), BF),
            pltpu.VMEM((NY, nb, 4 * nb), BF),
            pltpu.VMEM((NY, nb, 4 * nb), F32),
            dma((10,)),
            dma((2, 2)), dma((4, 2)), dma((4, 2)), dma((4, 2)),
            dma((4, 2, 2)), dma((2, 4, 2)), dma((4, 2)),
            dma((4,)), dma((NZ,)), dma((NZ,)),
            dma((3, NZ)), dma((2, NZ)), dma((NZ,)),
            dma((2, NZ)), dma((2, NZ)),
            dma((2,)), dma((2,)),
            dma((2, 8)), dma((2, 8)), dma((2, 8)), dma((2, 2, 4)),
            dma((8,)), dma((8,)), dma((4,)), dma((4,)),
            dma((4,)), dma((4,)),
        ],
        compiler_params=pltpu.CompilerParams(
            collective_id=0, has_side_effects=True, vmem_limit_bytes=60 * 2**20
        ),
    )(hidden_in, down_weight, keep_mask)
    layer_out = rows.transpose(2, 0, 1, 3).reshape(8, NY * NZ * nb)
    return layer_out, hessian


def solution(mesh):
    in_specs = (P("tok", "col"), P("col", "tok"), P("col", "tok"))
    out_specs = (P(("tok", "col"), None), P("col", "tok"))
    return jax.shard_map(body, mesh=mesh, in_specs=in_specs, out_specs=out_specs, check_vma=False)
```

time: 114 us -> 109 us (0.956)
  the two profiles are of different devices: /device:TPU:5 before, /device:TPU:1 now
where the time goes in v3:
time: 109 us
  Pallas kernels  105 us (96%)
  local copies, waits for them, and re-layouts  3.51 us (3%)
    pallas_call x1, Pallas kernels, body(): pl.pallas_call(lambda *refs: kernel(scaling, *refs), out_shape=(jax.Shape...  105 us

profile of v3, /device:TPU:1, one launch (start us, length us, event | category | flops | bytes accessed | tf_op | source)
XLA Modules:
  0.0 109.1 jit_solution(16946232155424323319)
XLA Ops:
  0.6 104.9 %shard_map.50 = (f32[144,576]{1,0:T(8,128)}, bf16[4,8,8,144]{3,2,1,0:T(8,128)(2,1)}) custom-call(bf16[256,1152]{1,0:T(8,128)(2,1)} %refs_0_.1, bf16[144,4608]{1,0:T(8,128)(2,1)} %refs_1_.1, s32[144,4608]{1,0:T(8,128)} %refs_2_.1), custom_call_target="tpu_custom_call" | custom-call | tf_op jit(solution)/shard_map/pallas_call | solution.py:499
  105.6 0.9 copy.5
  106.5 0.8 reshape.7
  107.3 1.7 %copy.7 = f32[144,576]{1,0:T(8,128)} copy(f32[144,576]{1,0:T(8,128)} %get-tuple-element.9) | data formatting | bytes 663552

commit v4 on v3

--- a/solution.py
+++ b/solution.py
@@ -21,7 +21,7 @@
     scaling,
     hid, wgt, msk,
     hout, lout,
-    hbuf, wbuf, mbuf, bsend, bfull, abuf, csend, crecv, nrecv, pbuf, zsend, zrecv,
+    hbuf, wbuf, mbuf, bsend, bfull, abuf, csend, crecv, nrecv, pbuf, qbuf, zsend, zrecv,
     lacc, lt, rows, cols, ls, lz, lrecv, hsend, hrecv, hacc,
     in_sem, y1s, y1r, xs_s, xs_r, y2s, y2r, y3s, bs, br, rel_s, cs, cr, nr, zs, zr,
     ts, tr, rs, rr, ccs, ccr, l1s, l1r, l2s, l2r, hs, hr,
@@ -243,22 +243,22 @@
         left = bfull[lo:hi].reshape((hi - lo) * nb, kb)
         return dot_nt(left, abuf[4 + lax.rem(x + e, NX)]).reshape(hi - lo, nb, ntok)
 
-    via_up = (0, 2, 4, 6, 7)
+    via_up, via_down = (0, 2, 4), (1, 3, 5)
 
     def products(e, lo, hi, order=None):
-        pbuf[lo:hi] = product(e, lo, hi)
+        qbuf[lo:hi] = product(e, lo, hi)
         for i in order or range(lo, hi):
             src, ssem = csend.at[e - 1, i], cs.at[e - 1, i]
             if e == 2:
-                csend[1, i] = pbuf[i].astype(BF)
-                to = lax.rem(x + (1 if i in via_up else NX - 1), NX)
+                csend[1, i] = qbuf[i].astype(BF)
+                to = lax.rem(x + (1 if i in via_up else NX - 1 if i in via_down else 2), NX)
                 remote(src, nrecv.at[i], ssem, nr.at[i], dev(to, k, y, z)).start()
                 continue
-            if (i in via_up) == (e == 1):
+            if i in (via_up if e == 1 else via_down):
                 arrived(nrecv.at[i], nr.at[i])
-                csend[e - 1, i] = (pbuf[i] + nrecv[i].astype(F32)).astype(BF)
+                csend[e - 1, i] = (qbuf[i] + nrecv[i].astype(F32)).astype(BF)
             else:
-                csend[e - 1, i] = pbuf[i].astype(BF)
+                csend[e - 1, i] = qbuf[i].astype(BF)
             remote(
                 src, crecv.at[e // 2, i], ssem, cr.at[e // 2, i], dev(lax.rem(x + e, NX), k, y, z)
             ).start()
@@ -271,14 +271,14 @@
     relay_tokens(1)
     tokens_here(2)
     products(2, 0, 3)
+    relay_tokens(3)
     weights(3, 5)
     products(2, 3, 5)
-    relay_tokens(3)
+    relay_tokens(0)
     weights(5, 7)
     products(2, 5, 7)
     tokens_here(1)
     products(1, 0, 7, order=(1, 2, 3, 4, 5, 6, 0))
-    relay_tokens(0)
     tokens_here(3)
     products(3, 0, 7, order=(1, 2, 3, 4, 5, 6, 0))
     tokens_here(0)
@@ -287,7 +287,11 @@
     def reduce_x(i):
         for side in range(2):
             arrived(crecv.at[side, i], cr.at[side, i])
-        return pbuf[i] + crecv[0, i].astype(F32) + crecv[1, i].astype(F32)
+        acc = pbuf[i] + crecv[0, i].astype(F32) + crecv[1, i].astype(F32)
+        if i not in via_up + via_down:
+            arrived(nrecv.at[i], nr.at[i])
+            acc = acc + nrecv[i].astype(F32)
+        return acc
 
     def reduce_send(i):
         zq = zpart(i)
@@ -302,14 +306,10 @@
     weights(7, 8)
     products(2, 7, 8)
     products(3, 7, 8)
-    reduce_send(2)
-    reduce_send(3)
-    reduce_send(4)
     products(1, 7, 8)
     pbuf[7] = product(0, 7, 8)[0]
-    reduce_send(5)
-    reduce_send(6)
-    reduce_send(7)
+    for i in (2, 3, 4, 5, 6, 7):
+        reduce_send(i)
     acc = reduce_x(0)
     for h in range(2):
         lacc[h] = acc[:, h * half : (h + 1) * half]
@@ -372,7 +372,6 @@
 
     reduce_z(0)
     reduce_z(1)
-    spread(0)
 
     ident = (
         lax.broadcasted_iota(jnp.int32, (ntok, ntok), 0)
@@ -384,6 +383,7 @@
         remote(ls.at[:, z2], lz.at[:, z], l1s.at[d], l1r.at[z], dev(x, k, y, z2)).start()
     lz[:, z] = ls[:, z]
 
+    spread(0)
     spread(1)
 
     for d in range(1, NZ):
@@ -412,16 +412,6 @@
         hsend[e - 1] = hacc[y2].astype(BF)
         remote(hsend.at[e - 1], hrecv.at[y], hs.at[e], hr.at[y], dev(x, k, y2, z)).start()
     hout[...] = hacc[y]
-    for e in (1, 3, 2):
-        ys = lax.rem(y + e, NY)
-        arrived(hrecv.at[ys], hr.at[ys])
-        hout[...] += hrecv[ys].astype(F32)
-
-    for d in range(1, NY):
-        ys = lax.rem(y + d, NY)
-        arrived(lrecv.at[ys], l2r.at[ys])
-    lout[...] = lrecv[...]
-
     for h in range(2):
 
         @pl.when(y != 2 * k + h)
@@ -486,6 +476,19 @@
 
     for d in range(1, NZ):
         sent(ls.at[:, 0], l1s.at[d])
+
+    for e in (1, 3, 2):
+        ys = lax.rem(y + e, NY)
+        arrived(hrecv.at[ys], hr.at[ys])
+        hout[...] += hrecv[ys].astype(F32)
+
+    for d in range(1, NY):
+        ys = lax.rem(y + d, NY)
+        arrived(lrecv.at[ys], l2r.at[ys])
+    for ys in range(NY):
+        for zq in range(NZ):
+            at = (ys * NZ + zq) * nb
+            lout[:, at : at + nb] = lrecv[ys, zq]
     for d in range(1, NY):
         sent(lz.at[0], l2s.at[d])
         sent(hsend.at[d - 1], hs.at[d])
@@ -496,11 +499,11 @@
     nb = down_weight.shape[0]
     scaling = 2.0 / (ntok * lax.axis_size("tok"))
     dma = pltpu.SemaphoreType.DMA
-    hessian, rows = pl.pallas_call(
+    hessian, layer_out = pl.pallas_call(
         lambda *refs: kernel(scaling, *refs),
         out_shape=(
             jax.ShapeDtypeStruct((nb, 4 * nb), F32),
-            jax.ShapeDtypeStruct((NY, NZ, 8, nb), BF),
+            jax.ShapeDtypeStruct((8, NY * NZ * nb), BF),
         ),
         in_specs=[pl.BlockSpec(memory_space=pl.ANY)] * 3,
         out_specs=(pl.BlockSpec(memory_space=pltpu.VMEM),) * 2,
@@ -514,6 +517,7 @@
             pltpu.VMEM((3, NZ, nb, ntok), BF),
             pltpu.VMEM((2, NZ, nb, ntok), BF),
             pltpu.VMEM((NZ, nb, ntok), BF),
+            pltpu.VMEM((NZ, nb, ntok), F32),
             pltpu.VMEM((NZ, nb, ntok), F32),
             pltpu.VMEM((2, NZ, nb, ntok // 2), BF),
             pltpu.VMEM((2, NZ, nb, ntok // 2), BF),
@@ -542,7 +546,6 @@
             collective_id=0, has_side_effects=True, vmem_limit_bytes=60 * 2**20
         ),
     )(hidden_in, down_weight, keep_mask)
-    layer_out = rows.transpose(2, 0, 1, 3).reshape(8, NY * NZ * nb)
     return layer_out, hessian
 
 

time: 109 us -> 106 us (0.972); the launches traced: 109 us -> 104 us
  Pallas kernels: 105 us -> 100 us
    pallas_call x1, Pallas kernels: 105 us -> 100 us  [body(): pl.pallas_call(lambda *refs: kernel(scaling, *refs), out_shape=(jax.Shape...]
    unnamed x1 -> x2, local copies, waits for them, and re-layouts: 1.75 us -> 3.27 us
where the time goes in v4:
time: 106 us; the launch traced here: 104 us
  Pallas kernels  100 us (94%)
  local copies, waits for them, and re-layouts  3.27 us (3%)
    pallas_call x1, Pallas kernels, body(): pl.pallas_call(lambda *refs: kernel(scaling, *refs), out_shape=(jax.Shape...  100 us
    unnamed x2, local copies, waits for them, and re-layouts  3.27 us

profile of v4, /device:TPU:1, one launch (start us, length us, event | category | flops | bytes accessed | tf_op | source)
XLA Modules:
  0.0 104.4 jit_solution(8288481834623769559)
XLA Ops:
  0.6 100.5 %shard_map.50 = (f32[144,576]{1,0:T(8,128)}, bf16[8,4608]{1,0:T(8,128)(2,1)}) custom-call(bf16[256,1152]{1,0:T(8,128)(2,1)} %refs_0_.1, bf16[144,4608]{1,0:T(8,128)(2,1)} %refs_1_.1, s32[144,4608]{1,0:T(8,128)} %refs_2_.1), custom_call_target="tpu_custom_call" | custom-call | tf_op jit(solution)/shard_map/pallas_call | solution.py:502
  101.1 1.5 %copy.7 = bf16[8,4608]{1,0:T(8,128)(2,1)} copy(bf16[8,4608]{1,0:T(8,128)(2,1)} %get-tuple-element.8) | data formatting | bytes 147456
  102.7 1.7 %copy.8 = f32[144,576]{1,0:T(8,128)} copy(f32[144,576]{1,0:T(8,128)} %get-tuple-element.9) | data formatting | bytes 663552

commit v5 on v4

--- a/solution.py
+++ b/solution.py
@@ -107,8 +107,6 @@
             pltpu.make_async_copy(msk.at[:, pl.ds(0, kb)], mbuf.at[j], in_sem.at[6 + j]),
         )
 
-    lax.fori_loop(0, 4, prune, 0)
-
     pl.semaphore_wait(bar, jnp.where(x == y, 24, 25))
 
     quarter = half // 2
@@ -158,6 +156,7 @@
 
         return 0
 
+    lax.fori_loop(0, 4, prune, 0)
     lax.fori_loop(0, NZ, hand_out, 0)
 
     order = (2, 1, 3, 0)
@@ -269,11 +268,10 @@
     relay_tokens(2)
     weights(0, 3)
     relay_tokens(1)
+    weights(3, 5)
     tokens_here(2)
-    products(2, 0, 3)
+    products(2, 0, 5)
     relay_tokens(3)
-    weights(3, 5)
-    products(2, 3, 5)
     relay_tokens(0)
     weights(5, 7)
     products(2, 5, 7)

time: 106 us -> 106 us (level)
  no operation moved by 1% of the time
where the time goes in v5:
time: 106 us; the launch traced here: 105 us
  Pallas kernels  101 us (95%)
  local copies, waits for them, and re-layouts  3.27 us (3%)
    pallas_call x1, Pallas kernels, body(): pl.pallas_call(lambda *refs: kernel(scaling, *refs), out_shape=(jax.Shape...  101 us
    unnamed x2, local copies, waits for them, and re-layouts  3.27 us

profile of v5, /device:TPU:1, one launch (start us, length us, event | category | flops | bytes accessed | tf_op | source)
XLA Modules:
  0.0 104.5 jit_solution(12804646973526692381)
XLA Ops:
  0.6 100.6 %shard_map.50 = (f32[144,576]{1,0:T(8,128)}, bf16[8,4608]{1,0:T(8,128)(2,1)}) custom-call(bf16[256,1152]{1,0:T(8,128)(2,1)} %refs_0_.1, bf16[144,4608]{1,0:T(8,128)(2,1)} %refs_1_.1, s32[144,4608]{1,0:T(8,128)} %refs_2_.1), custom_call_target="tpu_custom_call" | custom-call | tf_op jit(solution)/shard_map/pallas_call | solution.py:500
  101.3 1.5 %copy.7 = bf16[8,4608]{1,0:T(8,128)(2,1)} copy(bf16[8,4608]{1,0:T(8,128)(2,1)} %get-tuple-element.8) | data formatting | bytes 147456
  102.8 1.7 %copy.8 = f32[144,576]{1,0:T(8,128)} copy(f32[144,576]{1,0:T(8,128)} %get-tuple-element.9) | data formatting | bytes 663552
